TPU v7x, 256 devices: a whole 4x4x8 slice. The times are simulated.
256 devices in a mesh: ctx: 128 (over x, z, y), tp: 2 (over core).
Axes of the slice: x: 4, y: 4, z: 8, core: 2. Of those that a mesh axis runs over, the one named last changes fastest.
Arguments:
- queries: bfloat16 [24576, 32, 128], P('ctx', 'tp'), may hold values from -6 to 6
- key_vectors: bfloat16 [24576, 4, 128], P('ctx', 'tp'), may hold values from -6 to 6
- value_matrix: bfloat16 [24576, 4, 128], P('ctx', 'tp'), may hold values from -6 to 6
- grad_out: bfloat16 [24576, 32, 128], P('ctx', 'tp'), may hold values from -6 to 6
- doc_lengths: int32 [64], replicated, may hold values from 1 to 1345, 24576 in all
Outputs:
- grad_queries: bfloat16 [24576, 32, 128], P('ctx', 'tp')
- grad_keys: bfloat16 [24576, 4, 128], P('ctx', 'tp')
- grad_values: bfloat16 [24576, 4, 128], P('ctx', 'tp')
Inputs may be any that keep to these rules, and one draw needn't show every extreme that they name: `doc_lengths`: 64 document lengths that sum to 24576; the longest is exactly 1345.
All inputs are finite; a program needn't handle non-finite values.
Results may differ from a plain program's by a relative error of at most 0.0079.
Values may be sent and summed in bfloat16 or wider, within the bound.
A program may use at most 64 MiB of HBM per device.

v0:
```python
import jax
import jax.numpy as jnp
from jax import lax
from jax.sharding import PartitionSpec as P

SPAN_LOG = 3
WIN = 8
KBLOCK = 512


neg_fill = -1e30


def shifted(array, axis, by):
    length = lax.axis_size(axis)
    pairs = [(i, i + by) for i in range(length) if 0 <= i + by < length]
    return lax.ppermute(array, axis, pairs)


def doc_index(positions, lengths):
    doc_ends = jnp.cumsum(lengths)
    return jnp.sum((positions[:, None] >= doc_ends[None, :]).astype(jnp.int32), axis=1)


def fetch_window(stacked):
    window = stacked[None]
    for section_no in range(SPAN_LOG):
        arrived = shifted(window, "ctx", 2**section_no)
        window = jnp.concatenate([arrived, window], axis=0)
    return window


def return_window(partials):
    by_offset = partials[::-1]
    for section_no in range(SPAN_LOG - 1, -1, -1):
        stride = 2**section_no
        arrived = shifted(by_offset[stride:], "ctx", -stride)
        by_offset = by_offset[:stride] + arrived
    return by_offset[0]


def shards(queries, key_vectors, value_matrix, grad_out, doc_lengths):
    stripe = queries.shape[0]
    local_heads = queries.shape[1]
    head_dim = queries.shape[2]
    softmax_scale = head_dim ** (-0.5)
    stacked = jnp.stack([key_vectors, value_matrix], axis=1)
    window = fetch_window(stacked)
    head_groups = window.shape[3]
    repeat_factor = local_heads // head_groups
    key_span = window.shape[0] * stripe
    block_count = key_span // KBLOCK
    key_blocks = window[:, :, 0].reshape(block_count, KBLOCK, head_groups, head_dim)
    value_blocks = window[:, :, 1].reshape(block_count, KBLOCK, head_groups, head_dim)
    query_rows = queries.reshape(stripe, head_groups, repeat_factor, head_dim)
    grad_rows = grad_out.reshape(stripe, head_groups, repeat_factor, head_dim)
    ctx_index = lax.axis_index("ctx")
    query_pos = ctx_index * stripe + jnp.arange(stripe, dtype=jnp.int32)
    query_doc = doc_index(query_pos, doc_lengths)
    window_start = (ctx_index - (WIN - 1)) * stripe
    numbers = jnp.arange(block_count, dtype=jnp.int32)
    stats_shape = (head_groups, repeat_factor, stripe)

    def live_mask(number):
        key_pos = window_start + number * KBLOCK + jnp.arange(KBLOCK, dtype=jnp.int32)
        key_doc = doc_index(key_pos, doc_lengths)
        causal = (key_pos[None, :] <= query_pos[:, None]) & (key_pos[None, :] >= 0)
        return causal & (key_doc[None, :] == query_doc[:, None])

    def logits_of(key_block, live_pairs):
        raw_scores = (
            jnp.einsum("qgrd,kgd->grqk", query_rows, key_block, preferred_element_type=jnp.float32)
            * softmax_scale
        )
        return jnp.where(live_pairs, raw_scores, neg_fill)

    def max_step(carried, inputs):
        run_max, run_sum = carried
        key_block, number = inputs
        live_pairs = live_mask(number)
        logits = logits_of(key_block, live_pairs)
        new_max = jnp.maximum(run_max, jnp.max(logits, axis=-1))
        weights = jnp.where(live_pairs, jnp.exp(logits - new_max[..., None]), 0.0)
        return ((new_max, run_sum * jnp.exp(run_max - new_max) + jnp.sum(weights, axis=-1)), None)

    start_stats = (
        jnp.full(stats_shape, neg_fill, jnp.float32),
        jnp.zeros(stats_shape, jnp.float32),
    )
    (run_max, run_sum), unused = lax.scan(max_step, start_stats, (key_blocks, numbers))
    log_total = run_max + jnp.log(run_sum)

    def probs_of(key_block, live_pairs):
        return jnp.where(
            live_pairs, jnp.exp(logits_of(key_block, live_pairs) - log_total[..., None]), 0.0
        )

    def delta_step(carried, inputs):
        key_block, value_block, number = inputs
        live_pairs = live_mask(number)
        probs = probs_of(key_block, live_pairs)
        grad_probs = jnp.einsum(
            "qgrd,kgd->grqk", grad_rows, value_block, preferred_element_type=jnp.float32
        )
        return (carried + jnp.sum(probs * grad_probs, axis=-1), None)

    row_dots, unused = lax.scan(
        delta_step, jnp.zeros(stats_shape, jnp.float32), (key_blocks, value_blocks, numbers)
    )

    def grad_step(carried, inputs):
        key_block, value_block, number = inputs
        live_pairs = live_mask(number)
        probs = probs_of(key_block, live_pairs)
        grad_probs = jnp.einsum(
            "qgrd,kgd->grqk", grad_rows, value_block, preferred_element_type=jnp.float32
        )
        grad_scores = (probs * (grad_probs - row_dots[..., None])).astype(jnp.bfloat16)
        probs_low = probs.astype(jnp.bfloat16)
        query_grad = carried + jnp.einsum(
            "grqk,kgd->qgrd", grad_scores, key_block, preferred_element_type=jnp.float32
        )
        key_grad = (
            jnp.einsum(
                "grqk,qgrd->kgd", grad_scores, query_rows, preferred_element_type=jnp.float32
            )
            * softmax_scale
        )
        value_grad = jnp.einsum(
            "grqk,qgrd->kgd", probs_low, grad_rows, preferred_element_type=jnp.float32
        )
        return (query_grad, jnp.stack([key_grad, value_grad], axis=1))

    start_grad = jnp.zeros((stripe, head_groups, repeat_factor, head_dim), jnp.float32)
    query_grad, block_grads = lax.scan(grad_step, start_grad, (key_blocks, value_blocks, numbers))
    kv_partials = block_grads.reshape(window.shape[0], stripe, 2, head_groups, head_dim)
    owned = return_window(kv_partials)
    query_out = (
        (query_grad * softmax_scale).reshape(stripe, local_heads, head_dim).astype(jnp.bfloat16)
    )
    return (query_out, owned[:, 0].astype(jnp.bfloat16), owned[:, 1].astype(jnp.bfloat16))


def solution(mesh):
    in_specs = (
        P("ctx", "tp", None),
        P("ctx", "tp", None),
        P("ctx", "tp", None),
        P("ctx", "tp", None),
        P(),
    )
    out_specs = (P("ctx", "tp", None), P("ctx", "tp", None), P("ctx", "tp", None))
    return jax.shard_map(shards, mesh=mesh, in_specs=in_specs, out_specs=out_specs, check_vma=False)
```

profile of v0, /device:TPU:6, one launch (start us, length us, event | category | flops | bytes accessed | tf_op | source)
XLA Modules:
  0.0 203.9 jit_solution(9334669016939858736)
XLA Ops:
  1.6 3.5 %collective-permute-start = (bf16[1,192,2,2,128]{4,1,0,3,2:T(8,128)(2,1)S(1)}, bf16[1,192,2,2,128]{4,1,0,3,2:T(8,128)(2,1)S(1)}, u32[]{:S(2)}, u32[]{:S(2)}) collective-permute-start(bf16[1,192,2,2,128]{4,1,0,3,2:T(8,128)(2,1)S(1)} %maximum_bitcast_fusion.1), channel_id=1, source_target_pairs={{0,2},{2,4},{4,6},{6,8},{8,10},{10,12},{12,14},{14,16},{16,18},{18... | collective-permute-start | bytes 589832 | tf_op jit(solution)/shard_map/ppermute | solution.py:17
  5.1 11.9 %collective-permute-done = bf16[1,192,2,2,128]{4,1,0,3,2:T(8,128)(2,1)S(1)} collective-permute-done((bf16[1,192,2,2,128]{4,1,0,3,2:T(8,128)(2,1)S(1)}, bf16[1,192,2,2,128]{4,1,0,3,2:T(8,128)(2,1)S(1)}, u32[]{:S(2)}, u32[]{:S(2)}) %collective-permute-start) | collective-permute-done | bytes 196640 | tf_op jit(solution)/shard_map/ppermute | solution.py:17
  19.0 14.8 %collective-permute-done.1 = bf16[2,192,2,2,128]{4,1,0,3,2:T(8,128)(2,1)S(1)} collective-permute-done((bf16[2,192,2,2,128]{4,1,0,3,2:T(8,128)(2,1)S(1)}, bf16[2,192,2,2,128]{4,1,0,3,2:T(8,128)(2,1)S(1)}, u32[]{:S(2)}, u32[]{:S(2)}) %collective-permute-start.1) | collective-permute-done | bytes 393248 | tf_op jit(solution)/shard_map/ppermute | solution.py:17
  38.9 2.2 %copy.28 = bf16[192,16,128]{2,0,1:T(8,128)(2,1)} copy(bf16[192,16,128]{2,1,0:T(8,128)(2,1)} %param.14) | data formatting | bytes 1572864 | tf_op args[3]
  41.2 15.6 %collective-permute-done.2 = bf16[4,192,2,2,128]{4,1,0,3,2:T(8,128)(2,1)} collective-permute-done((bf16[4,192,2,2,128]{4,1,0,3,2:T(8,128)(2,1)}, bf16[4,192,2,2,128]{4,1,0,3,2:T(8,128)(2,1)}, u32[]{:S(2)}, u32[]{:S(2)}) %collective-permute-start.2) | collective-permute-done | bytes 786464 | tf_op jit(solution)/shard_map/ppermute | solution.py:17
  59.3 14.7 %while.43 = (s32[]{:T(128)}, f32[2,8,192]{2,1,0:T(8,128)S(1)}, f32[2,8,192]{2,1,0:T(8,128)S(1)}, s32[3]{0:T(128)S(1)}, s32[]{:T(128)}, /*index=5*/s32[1,64]{1,0:...) while((s32[]{:T(128)}, f32[2,8,192]{2,1,0:T(8,128)S(1)}, ...), condition=%wide.region_6.7_spmd.clone, body=%wide.region_2.6_spmd.clone.sunk | while | flops 415744192 | bytes 14100164 | solution.py:90
  62.1 2.1 %select_reduce_fusion.2 = f32[2,8,192]{2,1,0:T(8,128)S(1)} fusion(f32[2,512,192,8]{1,2,3,0:T(8,128)S(1)} %get-tuple-element.906, f32[2,8,192]{2,1,0:T(8,128)S(1)} %select_maximum_fusion.2, pred[192,512]{1,0:T(8,128)(4,1)S(1)} %compare_and_fusion.6), kind=kLoop, calls=%fused_computation.4.clone.1 | loop fusion | flops 7861248 | bytes 6414336 | tf_op jit(solution)/shard_map/while/body/eval_jaxpr/reduce_sum | solution.py:84
  67.0 2.1 %select_reduce_fusion.2 = f32[2,8,192]{2,1,0:T(8,128)S(1)} fusion(f32[2,512,192,8]{1,2,3,0:T(8,128)S(1)} %get-tuple-element.906, f32[2,8,192]{2,1,0:T(8,128)S(1)} %select_maximum_fusion.2, pred[192,512]{1,0:T(8,128)(4,1)S(1)} %compare_and_fusion.6), kind=kLoop, calls=%fused_computation.4.clone.1 | loop fusion | flops 7861248 | bytes 6414336 | tf_op jit(solution)/shard_map/while/body/eval_jaxpr/reduce_sum | solution.py:84
  74.1 18.5 %while.44 = (s32[]{:T(128)}, f32[2,8,192]{2,1,0:T(8,128)S(1)}, s32[3]{0:T(128)S(1)}, s32[]{:T(128)}, s32[1,64]{1,0:T(1,128)S(1)}, /*index=5*/s32[192]{0:T(256)S(...) while((s32[]{:T(128)}, f32[2,8,192]{2,1,0:T(8,128)S(1)}, ...), condition=%wide.region_10.11_spmd.clone, body=%wide.region_7.10_spmd.clone.sunk | while | flops 815239360 | bytes 18097904 | solution.py:107
  76.7 3.6 %fusion.96 = f32[2,8,192]{2,1,0:T(8,128)S(1)} fusion(f32[2,512,192,8]{1,2,3,0:T(8,128)S(1)} %fusion.95, f32[2,8,192]{2,1,0:T(8,128)S(1)} %get-tuple-element.1010, pred[192,512]{1,0:T(8,128)(4,1)S(1)} %compare_and_fusion.7, bf16[192,2,8,128]{3,0,2,1:T(8,128)(2,1)S(1)} %copy-done, bf16[3,512,2,128]{3,1,2,0:T(8,128)(2,1)} %get-tuple-element.1011, ...), kind=kOutput, calls=%fused_computation.19.clone.1 | convolution fusion | flops 412087296 | bytes 7462916 | tf_op jit(solution)/shard_map/while/body/eval_jaxpr/qgrd,kgd->grqk/dot_general | solution.py:102
  82.9 3.6 %fusion.96 = f32[2,8,192]{2,1,0:T(8,128)S(1)} fusion(f32[2,512,192,8]{1,2,3,0:T(8,128)S(1)} %fusion.95, f32[2,8,192]{2,1,0:T(8,128)S(1)} %get-tuple-element.1010, pred[192,512]{1,0:T(8,128)(4,1)S(1)} %compare_and_fusion.7, bf16[192,2,8,128]{3,0,2,1:T(8,128)(2,1)S(1)} %copy-done, bf16[3,512,2,128]{3,1,2,0:T(8,128)(2,1)} %get-tuple-element.1011, ...), kind=kOutput, calls=%fused_computation.19.clone.1 | convolution fusion | flops 412087296 | bytes 7462916 | tf_op jit(solution)/shard_map/while/body/eval_jaxpr/qgrd,kgd->grqk/dot_general | solution.py:102
  89.1 3.6 %fusion.96 = f32[2,8,192]{2,1,0:T(8,128)S(1)} fusion(f32[2,512,192,8]{1,2,3,0:T(8,128)S(1)} %fusion.95, f32[2,8,192]{2,1,0:T(8,128)S(1)} %get-tuple-element.1010, pred[192,512]{1,0:T(8,128)(4,1)S(1)} %compare_and_fusion.7, bf16[192,2,8,128]{3,0,2,1:T(8,128)(2,1)S(1)} %copy-done, bf16[3,512,2,128]{3,1,2,0:T(8,128)(2,1)} %get-tuple-element.1011, ...), kind=kOutput, calls=%fused_computation.19.clone.1 | convolution fusion | flops 412087296 | bytes 7462916 | tf_op jit(solution)/shard_map/while/body/eval_jaxpr/qgrd,kgd->grqk/dot_general | solution.py:102
  92.7 38.1 %while.45 = (s32[]{:T(128)}, f32[192,2,8,128]{3,0,2,1:T(8,128)S(1)}, f32[3,512,2,2,128]{4,1,0,3,2:T(8,128)}, bf16[3,512,2,128]{3,1,2,0:T(8,128)(2,1)S(1)}, s32[3...) while((s32[]{:T(128)}, ...), condition=%wide.region_13.14_spmd.clone, body=%wide.region_11.13_spmd.clone.sunk | while | flops 2033812736 | bytes 42026760 | solution.py:135
  95.3 2.7 %fusion.109 = f32[512,1,2,128]{3,0,2,1:T(8,128)S(1)} fusion(bf16[192,2,8,128]{3,0,2,1:T(8,128)(2,1)S(1)} %copy-done.1, f32[2,512,192,8]{1,2,3,0:T(8,128)S(1)} %fusion.107, f32[2,8,192]{2,1,0:T(8,128)S(1)} %get-tuple-element.1060, pred[192,512]{1,0:T(8,128)(4,1)S(1)} %compare_and_fusion.8), kind=kOutput, calls=%fused_computation.51.clone.1 | convolution fusion | flops 410517504 | bytes 7712768 | tf_op jit(solution)/shard_map/while/body/eval_jaxpr/grqk,qgrd->kgd/dot_general | solution.py:129
  98.0 3.6 %fusion.108 = bf16[2,8,192,512]{3,2,1,0:T(8,128)(2,1)S(1)} fusion(f32[2,512,192,8]{1,2,3,0:T(8,128)S(1)} %fusion.107, f32[2,8,192]{2,1,0:T(8,128)S(1)} %get-tuple-element.1063, f32[2,8,192]{2,1,0:T(8,128)S(1)} %get-tuple-element.1060, pred[192,512]{1,0:T(8,128)(4,1)S(1)} %compare_and_fusion.8, bf16[192,2,8,128]{3,0,2,1:T(8,128)(2,1)S(1)} %copy-done.1, ...), kind=kOutput, calls=%fused_computation.39.clone.1 | convolution fusion | flops 413663232 | bytes 10608644 | tf_op jit(solution)/shard_map/while/body/eval_jaxpr/qgrd,kgd->grqk/dot_general | solution.py:115
  107.9 2.7 %fusion.109 = f32[512,1,2,128]{3,0,2,1:T(8,128)S(1)} fusion(bf16[192,2,8,128]{3,0,2,1:T(8,128)(2,1)S(1)} %copy-done.1, f32[2,512,192,8]{1,2,3,0:T(8,128)S(1)} %fusion.107, f32[2,8,192]{2,1,0:T(8,128)S(1)} %get-tuple-element.1060, pred[192,512]{1,0:T(8,128)(4,1)S(1)} %compare_and_fusion.8), kind=kOutput, calls=%fused_computation.51.clone.1 | convolution fusion | flops 410517504 | bytes 7712768 | tf_op jit(solution)/shard_map/while/body/eval_jaxpr/grqk,qgrd->kgd/dot_general | solution.py:129
  110.7 3.6 %fusion.108 = bf16[2,8,192,512]{3,2,1,0:T(8,128)(2,1)S(1)} fusion(f32[2,512,192,8]{1,2,3,0:T(8,128)S(1)} %fusion.107, f32[2,8,192]{2,1,0:T(8,128)S(1)} %get-tuple-element.1063, f32[2,8,192]{2,1,0:T(8,128)S(1)} %get-tuple-element.1060, pred[192,512]{1,0:T(8,128)(4,1)S(1)} %compare_and_fusion.8, bf16[192,2,8,128]{3,0,2,1:T(8,128)(2,1)S(1)} %copy-done.1, ...), kind=kOutput, calls=%fused_computation.39.clone.1 | convolution fusion | flops 413663232 | bytes 10608644 | tf_op jit(solution)/shard_map/while/body/eval_jaxpr/qgrd,kgd->grqk/dot_general | solution.py:115
  120.6 2.7 %fusion.109 = f32[512,1,2,128]{3,0,2,1:T(8,128)S(1)} fusion(bf16[192,2,8,128]{3,0,2,1:T(8,128)(2,1)S(1)} %copy-done.1, f32[2,512,192,8]{1,2,3,0:T(8,128)S(1)} %fusion.107, f32[2,8,192]{2,1,0:T(8,128)S(1)} %get-tuple-element.1060, pred[192,512]{1,0:T(8,128)(4,1)S(1)} %compare_and_fusion.8), kind=kOutput, calls=%fused_computation.51.clone.1 | convolution fusion | flops 410517504 | bytes 7712768 | tf_op jit(solution)/shard_map/while/body/eval_jaxpr/grqk,qgrd->kgd/dot_general | solution.py:129
  123.4 3.6 %fusion.108 = bf16[2,8,192,512]{3,2,1,0:T(8,128)(2,1)S(1)} fusion(f32[2,512,192,8]{1,2,3,0:T(8,128)S(1)} %fusion.107, f32[2,8,192]{2,1,0:T(8,128)S(1)} %get-tuple-element.1063, f32[2,8,192]{2,1,0:T(8,128)S(1)} %get-tuple-element.1060, pred[192,512]{1,0:T(8,128)(4,1)S(1)} %compare_and_fusion.8, bf16[192,2,8,128]{3,0,2,1:T(8,128)(2,1)S(1)} %copy-done.1, ...), kind=kOutput, calls=%fused_computation.39.clone.1 | convolution fusion | flops 413663232 | bytes 10608644 | tf_op jit(solution)/shard_map/while/body/eval_jaxpr/qgrd,kgd->grqk/dot_general | solution.py:115
  130.8 3.3 %fusion.53 = (f32[4,192,2,2,128]{4,1,0,3,2:T(8,128)}, f32[4,192,2,2,128]{4,1,0,3,2:T(8,128)S(1)}) fusion(f32[8,192,2,2,128]{4,1,0,3,2:T(8,128)} %bitcast.205), kind=kLoop, calls=%fused_computation.90 | loop fusion | bytes 6291456 | tf_op jit(solution)/shard_map/slice | solution.py:38
  137.3 34.0 %collective-permute-done.3 = f32[4,192,2,2,128]{4,1,0,3,2:T(8,128)S(1)} collective-permute-done((f32[4,192,2,2,128]{4,1,0,3,2:T(8,128)}, f32[4,192,2,2,128]{4,1,0,3,2:T(8,128)S(1)}, u32[]{:S(2)}, u32[]{:S(2)}) %collective-permute-start.3) | collective-permute-done | bytes 1572896 | tf_op jit(solution)/shard_map/ppermute | solution.py:17
  174.9 17.6 %collective-permute-done.4 = f32[2,192,2,2,128]{4,1,0,3,2:T(8,128)S(1)} collective-permute-done((f32[2,192,2,2,128]{4,1,0,3,2:T(8,128)S(1)}, f32[2,192,2,2,128]{4,1,0,3,2:T(8,128)S(1)}, u32[]{:S(2)}, u32[]{:S(2)}) %collective-permute-start.4) | collective-permute-done | bytes 786464 | tf_op jit(solution)/shard_map/ppermute | solution.py:17
  192.7 2.5 %collective-permute-start.5 = (f32[1,192,2,2,128]{4,1,0,3,2:T(8,128)S(1)}, f32[1,192,2,2,128]{4,1,0,3,2:T(8,128)S(1)}, u32[]{:S(2)}, u32[]{:S(2)}) collective-permute-start(f32[1,192,2,2,128]{4,1,0,3,2:T(8,128)S(1)} %slice.57), channel_id=1, source_target_pairs={{2,0},{4,2},{6,4},{8,6},{10,8},{12,10},{14,12},{16,14},{18,16},{20... | collective-permute-start | bytes 1179656 | tf_op jit(solution)/shard_map/ppermute | solution.py:17
  196.8 5.5 %collective-permute-done.5 = f32[1,192,2,2,128]{4,1,0,3,2:T(8,128)S(1)} collective-permute-done((f32[1,192,2,2,128]{4,1,0,3,2:T(8,128)S(1)}, f32[1,192,2,2,128]{4,1,0,3,2:T(8,128)S(1)}, u32[]{:S(2)}, u32[]{:S(2)}) %collective-permute-start.5) | collective-permute-done | bytes 393248 | tf_op jit(solution)/shard_map/ppermute | solution.py:17
  (133 shorter events, 51.7 us)
Async XLA Ops:
  1.6 15.4 %collective-permute-start = (bf16[1,192,2,2,128]{4,1,0,3,2:T(8,128)(2,1)S(1)}, bf16[1,192,2,2,128]{4,1,0,3,2:T(8,128)(2,1)S(1)}, u32[]{:S(2)}, u32[]{:S(2)}) collective-permute-start(bf16[1,192,2,2,128]{4,1,0,3,2:T(8,128)(2,1)S(1)} %maximum_bitcast_fusion.1), channel_id=1, source_target_pairs={{0,2},{2,4},{4,6},{6,8},{8,10},{10,12},{12,14},{14,16},{16,18},{18... | collective-permute-start | bytes 589832 | tf_op jit(solution)/shard_map/ppermute | solution.py:17
  17.0 16.7 %collective-permute-start.1 = (bf16[2,192,2,2,128]{4,1,0,3,2:T(8,128)(2,1)S(1)}, bf16[2,192,2,2,128]{4,1,0,3,2:T(8,128)(2,1)S(1)}, u32[]{:S(2)}, u32[]{:S(2)}) collective-permute-start(bf16[2,192,2,2,128]{4,1,0,3,2:T(8,128)(2,1)S(1)} %pad_maximum_fusion.2), channel_id=1, source_target_pairs={{0,4},{2,6},{4,8},{6,10},{8,12},{10,14},{12,16},{14,18},{16,20},{1... | collective-permute-start | bytes 1179656 | tf_op jit(solution)/shard_map/ppermute | solution.py:17
  34.7 22.2 %collective-permute-start.2 = (bf16[4,192,2,2,128]{4,1,0,3,2:T(8,128)(2,1)}, bf16[4,192,2,2,128]{4,1,0,3,2:T(8,128)(2,1)}, u32[]{:S(2)}, u32[]{:S(2)}) collective-permute-start(bf16[4,192,2,2,128]{4,1,0,3,2:T(8,128)(2,1)} %pad_maximum_fusion.1), channel_id=1, source_target_pairs={{0,8},{2,10},{4,12},{6,14},{8,16},{10,18},{12,20},{14,22},{16,24},... | collective-permute-start | bytes 2359304 | tf_op jit(solution)/shard_map/ppermute | solution.py:17
  75.4 1.3 copy-start
  81.6 1.3 copy-start
  87.7 1.3 copy-start
  93.9 1.3 copy-start.1
  106.6 1.3 copy-start.1
  119.3 1.3 copy-start.1
  135.4 35.9 %collective-permute-start.3 = (f32[4,192,2,2,128]{4,1,0,3,2:T(8,128)}, f32[4,192,2,2,128]{4,1,0,3,2:T(8,128)S(1)}, u32[]{:S(2)}, u32[]{:S(2)}) collective-permute-start(f32[4,192,2,2,128]{4,1,0,3,2:T(8,128)} %slice.43), channel_id=1, source_target_pairs={{8,0},{10,2},{12,4},{14,6},{16,8},{18,10},{20,12},{22,14},{24,16},... | collective-permute-start | bytes 4718600 | tf_op jit(solution)/shard_map/ppermute | solution.py:17
  173.0 19.5 %collective-permute-start.4 = (f32[2,192,2,2,128]{4,1,0,3,2:T(8,128)S(1)}, f32[2,192,2,2,128]{4,1,0,3,2:T(8,128)S(1)}, u32[]{:S(2)}, u32[]{:S(2)}) collective-permute-start(f32[2,192,2,2,128]{4,1,0,3,2:T(8,128)S(1)} %slice.55), channel_id=1, source_target_pairs={{4,0},{6,2},{8,4},{10,6},{12,8},{14,10},{16,12},{18,14},{20,16},{2... | collective-permute-start | bytes 2359304 | tf_op jit(solution)/shard_map/ppermute | solution.py:17
  192.7 9.7 %collective-permute-start.5 = (f32[1,192,2,2,128]{4,1,0,3,2:T(8,128)S(1)}, f32[1,192,2,2,128]{4,1,0,3,2:T(8,128)S(1)}, u32[]{:S(2)}, u32[]{:S(2)}) collective-permute-start(f32[1,192,2,2,128]{4,1,0,3,2:T(8,128)S(1)} %slice.57), channel_id=1, source_target_pairs={{2,0},{4,2},{6,4},{8,6},{10,8},{12,10},{14,12},{16,14},{18,16},{20... | collective-permute-start | bytes 1179656 | tf_op jit(solution)/shard_map/ppermute | solution.py:17
where the time goes:
time: 205 us; the launch traced here: 204 us
  waiting for transfers between devices  99.5 us (49%)
  matrix products  47.2 us (23%)
  local copies, waits for them, and re-layouts  18.6 us (9%)
  other arithmetic  17.6 us (9%)
  starting transfers between devices  13.7 us (7%)
  loops' own time  6.54 us (3%)
    ppermute x6, waiting for transfers between devices, shifted(): return lax.ppermute(array, axis, pairs)  99.5 us
    ppermute x6, starting transfers between devices, shifted(): return lax.ppermute(array, axis, pairs)  13.7 us
    dot_general x3, matrix products, grad_step(): jnp.einsum('qgrd,kgd->grqk', grad_rows, value_block, preferred_element_ty...  10.7 us
    dot_general x3, matrix products, delta_step(): jnp.einsum('qgrd,kgd->grqk', grad_rows, value_block, preferred_element_ty...  10.7 us
    dot_general x9, matrix products, logits_of(): jnp.einsum('qgrd,kgd->grqk', query_rows, key_block, preferred_element_typ...  9.47 us
    dot_general x3, matrix products, grad_step(): jnp.einsum('grqk,qgrd->kgd', probs_low, grad_rows, preferred_element_type...  8.19 us
    reduce_sum x3, other arithmetic, max_step(): jnp.sum(weights, axis=-1)  6.27 us
    unnamed x6, local copies, waits for them, and re-layouts  6.02 us
  transfers between devices with their start and end apart: 6, of which 6 were waited for; matrix products, arithmetic and copies ran while one was open for 3% of the time, Pallas kernels for 0%

commit v1 on v0

v1 whole, which is shorter than its diff:
```python
import functools

import jax
import jax.numpy as jnp
from jax import lax
from jax.experimental import pallas as pl
from jax.experimental.pallas import tpu as pltpu
from jax.sharding import PartitionSpec as P

RING = 4
SLOTS = 8
FAN = 8
DIM = 128
QTILE = 256
GROUPS = 2
LOG2E = 1.4426950408889634
DEAD = -1e30


def program_order():
    a = lambda s, c: ("A", s, c)
    f = lambda s, g: ("F", s, g)
    b = lambda s, g: ("B", s, g)
    r = lambda s, g: ("R", s, g)
    return [
        f(0, 0), f(0, 1),
        a(4, 0), a(1, 0), a(4, 1), a(1, 1), f(4, 0),
        a(4, 2), a(1, 2), a(3, 0), f(1, 0),
        a(4, 3), a(1, 3), a(3, 1), a(5, 0), f(3, 0),
        f(4, 1), a(5, 1), a(3, 2), f(5, 0),
        a(3, 3), a(5, 2), a(7, 0), f(1, 1),
        a(5, 3), a(7, 1), a(2, 0), a(2, 1), f(7, 0),
        f(2, 0), a(7, 2), f(3, 1), a(7, 3), f(5, 1),
        a(6, 0), a(6, 1), f(6, 0), ("S", 0, 0), b(6, 0), r(6, 0),
        b(2, 0), r(2, 0), a(2, 2), a(2, 3), f(2, 1), f(7, 1),
        b(7, 0), b(5, 0), a(6, 2), a(6, 3), f(6, 1), ("S", 0, 1), b(6, 1), r(6, 1),
        r(7, 0), r(5, 0), b(2, 1), r(2, 1), b(3, 0), b(1, 0),
        b(7, 1), r(3, 0), r(1, 0), r(7, 1), b(5, 1), r(5, 1),
        b(4, 0), b(3, 1), b(1, 1), r(4, 0), r(3, 1), r(1, 1), b(0, 0),
        b(4, 1), r(4, 1), b(0, 1), ("Q", 0, 0), ("Q", 0, 1),
        r(0, 0), r(0, 1),
    ]


def kernel(
    tok, nctx, ndocs, q_hbm, k_hbm, v_hbm, do_hbm, len_ref, dq_hbm, dk_hbm, dv_hbm,
    qin, doin, kin, vin, wide, kv, qrow, qcol, orow, ocol, start_ref, pos_ref,
    mst, lst, dst_, prob, gprob, plow, dscore, grad, sbuf, rbuf, dqf, outk, outv, outq,
    in_sem, out_sem, fs_sem, fr_sem, rs_sem, rr_sem,
):
    me = lax.axis_index("ctx")
    y = lax.rem(me, RING)
    row = me - y
    up = row + lax.rem(y + 1, RING)
    down = row + lax.rem(y + RING - 1, RING)
    ahead = lax.rem(me + RING, nctx)
    behind = lax.rem(me + nctx - RING, nctx)
    qrows = tok * FAN
    tiles = qrows // QTILE
    scale = DIM**-0.5

    copies = [
        pltpu.make_async_copy(k_hbm, kin, in_sem.at[0]),
        pltpu.make_async_copy(v_hbm, vin, in_sem.at[1]),
        pltpu.make_async_copy(q_hbm, qin, in_sem.at[2]),
        pltpu.make_async_copy(do_hbm, doin, in_sem.at[3]),
    ]
    for copy in copies:
        copy.start()
    barrier = pltpu.get_barrier_semaphore()
    for other in (up, down, ahead, behind):
        pl.semaphore_signal(
            barrier, inc=1, device_id={"ctx": other}, device_id_type=pl.DeviceIdType.MESH
        )
    for which, source in enumerate((kin, vin)):
        copies[which].wait()
        wide[which] = source[...].astype(jnp.float32)
        for g in range(GROUPS):
            kv[g, which, 0:tok] = wide[which, pl.ds(g, tok, stride=GROUPS), :].astype(jnp.bfloat16)
    pl.semaphore_wait(barrier, 4)

    fetch = {
        1: (up, jnp.where(y < RING - 1, 0, 4)),
        2: (up, jnp.where(y < RING - 1, 1, 5)),
        3: (down, jnp.where(y > 0, 4, 0)),
        4: (ahead, 0),
        5: (ahead, 1),
        6: (down, jnp.where(y > 0, 7, 3)),
        7: (ahead, 3),
    }
    parent = {1: down, 2: down, 3: up, 4: behind, 5: behind, 6: up, 7: behind}

    def fetch_copy(slot, c):
        target, source = fetch[slot]
        g, which = c // 2, c % 2
        rows = pl.ds(pl.multiple_of(source * tok, 16), tok)
        return pltpu.make_async_remote_copy(
            src_ref=kv.at[g, which, rows],
            dst_ref=kv.at[g, which, pl.ds(slot * tok, tok)],
            send_sem=fs_sem.at[slot - 1, c],
            recv_sem=fr_sem.at[slot - 1, c],
            device_id={"ctx": target},
            device_id_type=pl.DeviceIdType.MESH,
        )

    def return_copy(slot, c):
        return pltpu.make_async_remote_copy(
            src_ref=sbuf.at[slot - 1, c],
            dst_ref=rbuf.at[slot - 1, c],
            send_sem=rs_sem.at[slot - 1, c],
            recv_sem=rr_sem.at[slot - 1, c],
            device_id={"ctx": parent[slot]},
            device_id_type=pl.DeviceIdType.MESH,
        )

    def start_if(condition, slot, c):
        if condition is None:
            fetch_copy(slot, c).start()
        else:

            @pl.when(condition)
            def _():
                fetch_copy(slot, c).start()

    for c in range(4):
        start_if(None, 4, c)
        start_if(y < RING - 1, 1, c)
        start_if(y == 0, 3, c)

    forwards = {
        1: ((5, None), (2, y < RING - 1)),
        4: ((1, y == RING - 1), (3, y > 0)),
        3: ((7, None), (6, y == 0)),
        5: ((2, y == RING - 1),),
        7: ((6, y > 0),),
        2: (),
        6: (),
    }

    def arrive(slot, c):
        fetch_copy(slot, c).wait_recv()
        for onward, condition in forwards[slot]:
            start_if(condition, onward, c)

    step = QTILE // FAN
    for which, (source, rows_ref, cols_ref) in enumerate(((qin, qrow, qcol), (doin, orow, ocol))):
        copies[2 + which].wait()

        @pl.loop(0, tok // step)
        def _(n):
            block = source[pl.ds(n * step, step)].astype(jnp.float32)
            at = pl.ds(pl.multiple_of(n * QTILE, QTILE), QTILE)
            for g in range(GROUPS):
                part = block[:, g * FAN : (g + 1) * FAN, :].reshape(QTILE, DIM)
                rows_ref[g, at, :] = part.astype(jnp.bfloat16)
                cols_ref[g, :, at] = part.T.astype(jnp.bfloat16)

    pos = me * tok + lax.shift_right_logical(lax.broadcasted_iota(jnp.int32, (1, qrows), 1), 3)

    def doc_step(n, carried):
        end, begin = carried
        end = end + len_ref[n]
        return end, jnp.where(pos >= end, end, begin)

    unused, begin = lax.fori_loop(0, ndocs, doc_step, (jnp.int32(0), jnp.zeros_like(pos)))
    start_ref[...] = begin
    pos_ref[...] = pos

    last = {0: None, 1: None}

    def first_pass(slot, g):
        rows = slice(slot * tok, (slot + 1) * tok)
        keys, values = kv[g, 0, rows], kv[g, 1, rows]
        before = last[g]
        key_pos = (me - slot) * tok + lax.broadcasted_iota(jnp.int32, (tok, QTILE), 0)
        for n in range(tiles):
            at = slice(n * QTILE, (n + 1) * QTILE)
            scores = jnp.dot(keys, qcol[g, :, at], preferred_element_type=jnp.float32)
            grads = jnp.dot(values, ocol[g, :, at], preferred_element_type=jnp.float32)
            live = key_pos >= start_ref[:, at]
            if slot == 0:
                live = live & (key_pos <= pos_ref[:, at])
            scores = jnp.where(live, scores * (scale * LOG2E), DEAD)
            top = jnp.max(scores, axis=0, keepdims=True)
            if before is not None:
                old = mst[g, before : before + 1, at]
                top = jnp.maximum(top, old)
            probs = jnp.exp2(scores - top)
            total = jnp.sum(probs, axis=0, keepdims=True)
            dots = jnp.sum(probs * grads, axis=0, keepdims=True)
            if before is not None:
                shrink = jnp.exp2(old - top)
                total = total + lst[g : g + 1, at] * shrink
                dots = dots + dst_[g : g + 1, at] * shrink
            mst[g, slot : slot + 1, at] = top
            lst[g : g + 1, at] = total
            dst_[g : g + 1, at] = dots
            prob[g, rows, at] = probs
            gprob[g, rows, at] = grads
        last[g] = slot

    def statistics(g):
        inverse = 1.0 / lst[g : g + 1, :]
        final = mst[g, last[g] : last[g] + 1, :]
        dst_[g : g + 1, :] = dst_[g : g + 1, :] * inverse
        for slot in range(SLOTS):
            mst[g, slot : slot + 1, :] = jnp.exp2(mst[g, slot : slot + 1, :] - final) * inverse

    def second_pass(slot, g):
        rows = slice(slot * tok, (slot + 1) * tok)
        key_sum, value_sum = None, None
        for n in range(tiles):
            at = slice(n * QTILE, (n + 1) * QTILE)
            probs = prob[g, rows, at] * mst[g, slot : slot + 1, at]
            scores = probs * (gprob[g, rows, at] - dst_[g : g + 1, at])
            low, scores = probs.astype(jnp.bfloat16), scores.astype(jnp.bfloat16)
            dscore[g, rows, at] = scores
            value_part = jnp.dot(low, orow[g, at, :], preferred_element_type=jnp.float32)
            key_part = jnp.dot(scores, qrow[g, at, :], preferred_element_type=jnp.float32)
            key_sum = key_part if n == 0 else key_sum + key_part
            value_sum = value_part if n == 0 else value_sum + value_part
        if slot in (2, 6):
            sbuf[slot - 1, 2 * g] = key_sum.astype(jnp.bfloat16)
            sbuf[slot - 1, 2 * g + 1] = value_sum.astype(jnp.bfloat16)
        else:
            grad[slot, 2 * g] = key_sum
            grad[slot, 2 * g + 1] = value_sum

    takes = {
        7: ((6, y > 0),),
        5: ((2, y == RING - 1),),
        3: ((7, None), (6, y == 0)),
        1: ((5, None), (2, y < RING - 1)),
        4: ((1, y == RING - 1), (3, y > 0)),
        0: ((4, None), (1, y < RING - 1), (3, y == 0)),
    }

    def take(slot, given, c):
        return_copy(given, c).wait_recv()
        grad[slot, c] = grad[slot, c] + rbuf[given - 1, c].astype(jnp.float32)

    def give_back(slot, g):
        for c in (2 * g, 2 * g + 1):
            for given, condition in takes.get(slot, ()):
                if condition is None:
                    take(slot, given, c)
                else:
                    pl.when(condition)(functools.partial(take, slot, given, c))
            if slot in takes and slot > 0:
                sbuf[slot - 1, c] = grad[slot, c].astype(jnp.bfloat16)
            if slot > 0:
                return_copy(slot, c).start()

    def query_grads(g):
        for n in range(tiles):
            at = slice(n * QTILE, (n + 1) * QTILE)
            part = lax.dot_general(
                dscore[g, :, at], kv[g, 0], (((0,), (0,)), ((), ())),
                preferred_element_type=jnp.float32,
            )
            dqf[g, at, :] = part * scale

    acts = {
        "A": arrive, "F": first_pass, "B": second_pass, "R": give_back,
        "S": lambda unused, g: statistics(g), "Q": lambda unused, g: query_grads(g),
    }
    for kind, slot, which in program_order():
        if kind == "R" and slot == 0 and which == 0:

            @pl.loop(0, tok // step)
            def _(n):
                at = pl.ds(pl.multiple_of(n * QTILE, QTILE), QTILE)
                parts = [dqf[g, at, :].reshape(step, FAN, DIM) for g in range(GROUPS)]
                outq[pl.ds(n * step, step)] = jnp.concatenate(parts, axis=1).astype(jnp.bfloat16)

            out_q = pltpu.make_async_copy(outq, dq_hbm, out_sem.at[2])
            out_q.start()
        acts[kind](slot, which)

    for g in range(GROUPS):
        wide[0, pl.ds(g, tok, stride=GROUPS), :] = grad[0, 2 * g] * scale
        wide[1, pl.ds(g, tok, stride=GROUPS), :] = grad[0, 2 * g + 1]
    outk[...] = wide[0].astype(jnp.bfloat16)
    outv[...] = wide[1].astype(jnp.bfloat16)
    out_k = pltpu.make_async_copy(outk, dk_hbm, out_sem.at[0])
    out_v = pltpu.make_async_copy(outv, dv_hbm, out_sem.at[1])
    out_k.start()
    out_v.start()
    for slot in range(1, SLOTS):
        for c in range(4):
            fetch_copy(slot, c).wait_send()
            return_copy(slot, c).wait_send()
    out_q.wait()
    out_k.wait()
    out_v.wait()


def local(nctx, queries, key_vectors, value_matrix, grad_out, doc_lengths):
    tok, heads, dim = queries.shape
    qrows = tok * FAN
    bf, f32 = jnp.bfloat16, jnp.float32
    anywhere = pl.BlockSpec(memory_space=pl.ANY)
    dq, dk, dv = pl.pallas_call(
        functools.partial(kernel, tok, nctx, doc_lengths.shape[0]),
        out_shape=(
            jax.ShapeDtypeStruct((tok, heads, dim), bf),
            jax.ShapeDtypeStruct((tok * GROUPS, dim), bf),
            jax.ShapeDtypeStruct((tok * GROUPS, dim), bf),
        ),
        in_specs=[anywhere] * 4 + [pl.BlockSpec(memory_space=pltpu.SMEM)],
        out_specs=(anywhere,) * 3,
        scratch_shapes=[
            pltpu.VMEM((tok, heads, dim), bf),
            pltpu.VMEM((tok, heads, dim), bf),
            pltpu.VMEM((tok * GROUPS, dim), bf),
            pltpu.VMEM((tok * GROUPS, dim), bf),
            pltpu.VMEM((2, tok * GROUPS, dim), f32),
            pltpu.VMEM((GROUPS, 2, SLOTS * tok, dim), bf),
            pltpu.VMEM((GROUPS, qrows, dim), bf),
            pltpu.VMEM((GROUPS, dim, qrows), bf),
            pltpu.VMEM((GROUPS, qrows, dim), bf),
            pltpu.VMEM((GROUPS, dim, qrows), bf),
            pltpu.VMEM((1, qrows), jnp.int32),
            pltpu.VMEM((1, qrows), jnp.int32),
            pltpu.VMEM((GROUPS, SLOTS, qrows), f32),
            pltpu.VMEM((GROUPS, qrows), f32),
            pltpu.VMEM((GROUPS, qrows), f32),
            pltpu.VMEM((GROUPS, SLOTS * tok, qrows), f32),
            pltpu.VMEM((GROUPS, SLOTS * tok, qrows), f32),
            pltpu.VMEM((8, 128), bf),
            pltpu.VMEM((GROUPS, SLOTS * tok, qrows), bf),
            pltpu.VMEM((SLOTS, 4, tok, dim), f32),
            pltpu.VMEM((SLOTS - 1, 4, tok, dim), bf),
            pltpu.VMEM((SLOTS - 1, 4, tok, dim), bf),
            pltpu.VMEM((GROUPS, qrows, dim), f32),
            pltpu.VMEM((tok * GROUPS, dim), bf),
            pltpu.VMEM((tok * GROUPS, dim), bf),
            pltpu.VMEM((tok, heads, dim), bf),
            pltpu.SemaphoreType.DMA((4,)),
            pltpu.SemaphoreType.DMA((3,)),
            pltpu.SemaphoreType.DMA((SLOTS - 1, 4)),
            pltpu.SemaphoreType.DMA((SLOTS - 1, 4)),
            pltpu.SemaphoreType.DMA((SLOTS - 1, 4)),
            pltpu.SemaphoreType.DMA((SLOTS - 1, 4)),
        ],
        compiler_params=pltpu.CompilerParams(
            collective_id=0, has_side_effects=True, vmem_limit_bytes=67_043_328
        ),
    )(
        queries,
        key_vectors.reshape(tok * GROUPS, dim),
        value_matrix.reshape(tok * GROUPS, dim),
        grad_out,
        doc_lengths,
    )
    return dq, dk.reshape(tok, GROUPS, dim), dv.reshape(tok, GROUPS, dim)


def solution(mesh):
    spec = P("ctx", "tp", None)
    return jax.shard_map(
        functools.partial(local, mesh.shape["ctx"]),
        mesh=mesh,
        in_specs=(spec, spec, spec, spec, P()),
        out_specs=(spec, spec, spec),
        check_vma=False,
    )
```

time: 205 us -> 55.9 us (0.27)
  the two profiles are of different devices: /device:TPU:6 before, /device:TPU:24 now
where the time goes in v1:
time: 55.9 us; the launch traced here: 55.7 us
  Pallas kernels  51.3 us (92%)
  local copies, waits for them, and re-layouts  3.75 us (7%)
  between operations  0.65 us (1%)
    pallas_call x1, Pallas kernels, local(): pl.pallas_call(functools.partial(kernel, tok, nctx, doc_lengths.shape[0])...  51.3 us
    unnamed x7, local copies, waits for them, and re-layouts  3.75 us

profile of v1, /device:TPU:24, one launch (start us, length us, event | category | flops | bytes accessed | tf_op | source)
XLA Modules:
  0.0 55.7 jit_solution(18255713365399500389)
XLA Ops:
  0.6 51.3 %shard_map.76 = (bf16[192,16,128]{2,1,0:T(8,128)(2,1)}, bf16[384,128]{1,0:T(8,128)(2,1)}, bf16[384,128]{1,0:T(8,128)(2,1)}) custom-call(bf16[192,16,128]{2,1,0:T(8,128)(2,1)} %q_hbm.1, bf16[384,128]{1,0:T(8,128)(2,1)} %bitcast.6, bf16[384,128]{1,0:T(8,128)(2,1)} %bitcast.7, bf16[192,16,128]{2,1,0:T(8,128)(2,1)} %do_hbm.1, s32[64]{0:T(128)} %len_ref.1), custom_call_target="tpu_custom_call" | custom-call | tf_op jit(solution)/shard_map/pallas_call | solution.py:303
  51.9 0.0 copy-start.1
  51.9 2.2 %copy.11 = bf16[192,16,128]{2,1,0:T(8,128)(2,1)} copy(bf16[192,16,128]{2,1,0:T(8,128)(2,1)} %get-tuple-element.12) | data formatting | bytes 1572864
  54.1 0.0 copy-done.1
  54.1 0.0 copy-start
  54.1 0.6 %copy.12 = bf16[192,2,128]{2,1,0:T(2,128)(2,1)} copy(bf16[192,2,128]{2,1,0:T(2,128)(2,1)S(1)} %bitcast.5) | data formatting | bytes 196608
  54.8 0.3 copy-done
  55.1 0.6 %copy.13 = bf16[192,2,128]{2,1,0:T(2,128)(2,1)} copy(bf16[192,2,128]{2,1,0:T(2,128)(2,1)S(1)} %bitcast.4) | data formatting | bytes 196608
Async XLA Ops:
  51.9 2.2 %copy-start.1 = (bf16[384,128]{1,0:T(8,128)(2,1)S(1)}, bf16[384,128]{1,0:T(8,128)(2,1)}, u32[]{:S(2)}) copy-start(bf16[384,128]{1,0:T(8,128)(2,1)} %get-tuple-element.7) | copy-start | bytes 294916
  54.1 0.9 %copy-start = (bf16[384,128]{1,0:T(8,128)(2,1)S(1)}, bf16[384,128]{1,0:T(8,128)(2,1)}, u32[]{:S(2)}) copy-start(bf16[384,128]{1,0:T(8,128)(2,1)} %get-tuple-element.8) | copy-start | bytes 294916

commit v2 on v1

--- a/solution.py
+++ b/solution.py
@@ -17,36 +17,23 @@
 DEAD = -1e30
 
 
-def program_order():
-    a = lambda s, c: ("A", s, c)
-    f = lambda s, g: ("F", s, g)
-    b = lambda s, g: ("B", s, g)
-    r = lambda s, g: ("R", s, g)
-    return [
-        f(0, 0), f(0, 1),
-        a(4, 0), a(1, 0), a(4, 1), a(1, 1), f(4, 0),
-        a(4, 2), a(1, 2), a(3, 0), f(1, 0),
-        a(4, 3), a(1, 3), a(3, 1), a(5, 0), f(3, 0),
-        f(4, 1), a(5, 1), a(3, 2), f(5, 0),
-        a(3, 3), a(5, 2), a(7, 0), f(1, 1),
-        a(5, 3), a(7, 1), a(2, 0), a(2, 1), f(7, 0),
-        f(2, 0), a(7, 2), f(3, 1), a(7, 3), f(5, 1),
-        a(6, 0), a(6, 1), f(6, 0), ("S", 0, 0), b(6, 0), r(6, 0),
-        b(2, 0), r(2, 0), a(2, 2), a(2, 3), f(2, 1), f(7, 1),
-        b(7, 0), b(5, 0), a(6, 2), a(6, 3), f(6, 1), ("S", 0, 1), b(6, 1), r(6, 1),
-        r(7, 0), r(5, 0), b(2, 1), r(2, 1), b(3, 0), b(1, 0),
-        b(7, 1), r(3, 0), r(1, 0), r(7, 1), b(5, 1), r(5, 1),
-        b(4, 0), b(3, 1), b(1, 1), r(4, 0), r(3, 1), r(1, 1), b(0, 0),
-        b(4, 1), r(4, 1), b(0, 1), ("Q", 0, 0), ("Q", 0, 1),
-        r(0, 0), r(0, 1),
-    ]
+KINDS = ("A", "P", "F", "S", "B", "R", "Q", "O")
+ORDER = (
+    0, 1, 2, 3, 100, 201, 40, 200, 41, 10, 240, 11, 42, 210, 30, 31, 12, 230,
+    43, 50, 32, 241, 51, 250, 70, 33, 231, 13, 71, 211, 21, 20, 220, 60, 52, 270,
+    61, 260, 300, 72, 460, 561, 450, 73, 420, 520, 470, 53, 560, 271, 22, 430, 521, 571,
+    62, 251, 63, 550, 261, 570, 23, 221, 301, 461, 563, 562, 551, 421, 523, 522, 401, 440,
+    471, 573, 531, 451, 553, 410, 511, 572, 431, 552, 530, 441, 411, 510, 400, 630, 533, 541,
+    540, 640, 601, 600, 513, 532, 621, 543, 512, 611, 542, 650, 500, 610, 641, 631, 651, 620,
+    700, 501, 503, 502,
+)
 
 
 def kernel(
-    tok, nctx, ndocs, q_hbm, k_hbm, v_hbm, do_hbm, len_ref, dq_hbm, dk_hbm, dv_hbm,
+    tok, nctx, ndocs, q_hbm, k_hbm, v_hbm, do_hbm, len_ref, dq_ref, dk_ref, dv_ref,
     qin, doin, kin, vin, wide, kv, qrow, qcol, orow, ocol, start_ref, pos_ref,
-    mst, lst, dst_, prob, gprob, plow, dscore, grad, sbuf, rbuf, dqf, outk, outv, outq,
-    in_sem, out_sem, fs_sem, fr_sem, rs_sem, rr_sem,
+    mst, lst, dst_, prob, gprob, dscore, grad, sbuf, rbuf, dqf,
+    in_sem, fs_sem, fr_sem, rs_sem, rr_sem,
 ):
     me = lax.axis_index("ctx")
     y = lax.rem(me, RING)
@@ -122,12 +109,8 @@
             def _():
                 fetch_copy(slot, c).start()
 
-    for c in range(4):
-        start_if(None, 4, c)
-        start_if(y < RING - 1, 1, c)
-        start_if(y == 0, 3, c)
-
     forwards = {
+        0: ((4, None), (1, y < RING - 1), (3, y == 0)),
         1: ((5, None), (2, y < RING - 1)),
         4: ((1, y == RING - 1), (3, y > 0)),
         3: ((7, None), (6, y == 0)),
@@ -138,33 +121,39 @@
     }
 
     def arrive(slot, c):
-        fetch_copy(slot, c).wait_recv()
+        if slot > 0:
+            fetch_copy(slot, c).wait_recv()
         for onward, condition in forwards[slot]:
             start_if(condition, onward, c)
 
     step = QTILE // FAN
-    for which, (source, rows_ref, cols_ref) in enumerate(((qin, qrow, qcol), (doin, orow, ocol))):
-        copies[2 + which].wait()
-
-        @pl.loop(0, tok // step)
-        def _(n):
-            block = source[pl.ds(n * step, step)].astype(jnp.float32)
-            at = pl.ds(pl.multiple_of(n * QTILE, QTILE), QTILE)
-            for g in range(GROUPS):
-                part = block[:, g * FAN : (g + 1) * FAN, :].reshape(QTILE, DIM)
-                rows_ref[g, at, :] = part.astype(jnp.bfloat16)
-                cols_ref[g, :, at] = part.T.astype(jnp.bfloat16)
-
-    pos = me * tok + lax.shift_right_logical(lax.broadcasted_iota(jnp.int32, (1, qrows), 1), 3)
-
-    def doc_step(n, carried):
-        end, begin = carried
-        end = end + len_ref[n]
-        return end, jnp.where(pos >= end, end, begin)
-
-    unused, begin = lax.fori_loop(0, ndocs, doc_step, (jnp.int32(0), jnp.zeros_like(pos)))
-    start_ref[...] = begin
-    pos_ref[...] = pos
+
+    def prepare():
+        sources = ((qin, qrow, qcol), (doin, orow, ocol))
+        for which, (source, rows_ref, cols_ref) in enumerate(sources):
+            copies[2 + which].wait()
+
+            @pl.loop(0, tok // step)
+            def _(n):
+                block = source[pl.ds(n * step, step)].astype(jnp.float32)
+                at = pl.ds(pl.multiple_of(n * QTILE, QTILE), QTILE)
+                for g in range(GROUPS):
+                    part = block[:, g * FAN : (g + 1) * FAN, :].reshape(QTILE, DIM)
+                    rows_ref[g, at, :] = part.astype(jnp.bfloat16)
+                    cols_ref[g, :, at] = part.T.astype(jnp.bfloat16)
+
+        pos = lax.broadcasted_iota(jnp.int32, (1, qrows), 1)
+        pos = me * tok + lax.shift_right_logical(pos, 3)
+
+        def doc_step(n, carried):
+            end, begin = carried
+            end = end + len_ref[n]
+            return end, jnp.where(pos >= end, end, begin)
+
+        empty = (jnp.int32(0), jnp.zeros_like(pos))
+        unused, begin = lax.fori_loop(0, ndocs, doc_step, empty)
+        start_ref[...] = begin
+        pos_ref[...] = pos
 
     last = {0: None, 1: None}
 
@@ -239,76 +228,73 @@
         return_copy(given, c).wait_recv()
         grad[slot, c] = grad[slot, c] + rbuf[given - 1, c].astype(jnp.float32)
 
-    def give_back(slot, g):
-        for c in (2 * g, 2 * g + 1):
-            for given, condition in takes.get(slot, ()):
-                if condition is None:
-                    take(slot, given, c)
-                else:
-                    pl.when(condition)(functools.partial(take, slot, given, c))
-            if slot in takes and slot > 0:
-                sbuf[slot - 1, c] = grad[slot, c].astype(jnp.bfloat16)
-            if slot > 0:
-                return_copy(slot, c).start()
-
-    def query_grads(g):
-        for n in range(tiles):
-            at = slice(n * QTILE, (n + 1) * QTILE)
-            part = lax.dot_general(
-                dscore[g, :, at], kv[g, 0], (((0,), (0,)), ((), ())),
-                preferred_element_type=jnp.float32,
-            )
-            dqf[g, at, :] = part * scale
+    def give_back(slot, c):
+        for given, condition in takes.get(slot, ()):
+            if condition is None:
+                take(slot, given, c)
+            else:
+                pl.when(condition)(functools.partial(take, slot, given, c))
+        if slot in takes and slot > 0:
+            sbuf[slot - 1, c] = grad[slot, c].astype(jnp.bfloat16)
+        if slot > 0:
+            return_copy(slot, c).start()
+
+    def query_grads(n, g):
+        at = slice(n * QTILE, (n + 1) * QTILE)
+        part = lax.dot_general(
+            dscore[g, :, at], kv[g, 0], (((0,), (0,)), ((), ())),
+            preferred_element_type=jnp.float32,
+        )
+        dqf[g, at, :] = part * scale
+
+    def write_queries():
+        @pl.loop(0, tok // step)
+        def _(n):
+            at = pl.ds(pl.multiple_of(n * QTILE, QTILE), QTILE)
+            parts = [dqf[g, at, :].reshape(step, FAN, DIM) for g in range(GROUPS)]
+            dq_ref[pl.ds(n * step, step)] = jnp.concatenate(parts, axis=1).astype(jnp.bfloat16)
 
     acts = {
-        "A": arrive, "F": first_pass, "B": second_pass, "R": give_back,
-        "S": lambda unused, g: statistics(g), "Q": lambda unused, g: query_grads(g),
+        "P": lambda unused, none: prepare(), "A": arrive, "F": first_pass, "B": second_pass,
+        "S": lambda unused, g: statistics(g), "Q": query_grads, "R": give_back,
+        "O": lambda unused, none: write_queries(),
     }
-    for kind, slot, which in program_order():
-        if kind == "R" and slot == 0 and which == 0:
-
-            @pl.loop(0, tok // step)
-            def _(n):
-                at = pl.ds(pl.multiple_of(n * QTILE, QTILE), QTILE)
-                parts = [dqf[g, at, :].reshape(step, FAN, DIM) for g in range(GROUPS)]
-                outq[pl.ds(n * step, step)] = jnp.concatenate(parts, axis=1).astype(jnp.bfloat16)
-
-            out_q = pltpu.make_async_copy(outq, dq_hbm, out_sem.at[2])
-            out_q.start()
-        acts[kind](slot, which)
+    for code in ORDER:
+        kind, rest = KINDS[code // 100], code % 100
+        if kind != "Q" or rest // 10 < tiles:
+            acts[kind](rest // 10, rest % 10)
 
     for g in range(GROUPS):
         wide[0, pl.ds(g, tok, stride=GROUPS), :] = grad[0, 2 * g] * scale
         wide[1, pl.ds(g, tok, stride=GROUPS), :] = grad[0, 2 * g + 1]
-    outk[...] = wide[0].astype(jnp.bfloat16)
-    outv[...] = wide[1].astype(jnp.bfloat16)
-    out_k = pltpu.make_async_copy(outk, dk_hbm, out_sem.at[0])
-    out_v = pltpu.make_async_copy(outv, dv_hbm, out_sem.at[1])
-    out_k.start()
-    out_v.start()
+    dk_ref[...] = wide[0].astype(jnp.bfloat16)
+    dv_ref[...] = wide[1].astype(jnp.bfloat16)
     for slot in range(1, SLOTS):
         for c in range(4):
             fetch_copy(slot, c).wait_send()
             return_copy(slot, c).wait_send()
-    out_q.wait()
-    out_k.wait()
-    out_v.wait()
-
+
+
+def writer(a, b, c, out_a, out_b, out_c, sem):
+    pairs = ((a, out_a), (b, out_b), (c, out_c))
+    copies = [pltpu.make_async_copy(x, o, sem.at[i]) for i, (x, o) in enumerate(pairs)]
+    for copy in copies:
+        copy.start()
+    for copy in copies:
+        copy.wait()
 
 def local(nctx, queries, key_vectors, value_matrix, grad_out, doc_lengths):
     tok, heads, dim = queries.shape
     qrows = tok * FAN
     bf, f32 = jnp.bfloat16, jnp.float32
     anywhere = pl.BlockSpec(memory_space=pl.ANY)
-    dq, dk, dv = pl.pallas_call(
+    shapes = ((tok, heads, dim), (tok * GROUPS, dim), (tok * GROUPS, dim))
+    inside = pl.BlockSpec(memory_space=pltpu.VMEM)
+    parts = pl.pallas_call(
         functools.partial(kernel, tok, nctx, doc_lengths.shape[0]),
-        out_shape=(
-            jax.ShapeDtypeStruct((tok, heads, dim), bf),
-            jax.ShapeDtypeStruct((tok * GROUPS, dim), bf),
-            jax.ShapeDtypeStruct((tok * GROUPS, dim), bf),
-        ),
+        out_shape=tuple(pltpu.VMEM(shape, bf) for shape in shapes),
         in_specs=[anywhere] * 4 + [pl.BlockSpec(memory_space=pltpu.SMEM)],
-        out_specs=(anywhere,) * 3,
+        out_specs=(inside,) * 3,
         scratch_shapes=[
             pltpu.VMEM((tok, heads, dim), bf),
             pltpu.VMEM((tok, heads, dim), bf),
@@ -327,24 +313,19 @@
             pltpu.VMEM((GROUPS, qrows), f32),
             pltpu.VMEM((GROUPS, SLOTS * tok, qrows), f32),
             pltpu.VMEM((GROUPS, SLOTS * tok, qrows), f32),
-            pltpu.VMEM((8, 128), bf),
             pltpu.VMEM((GROUPS, SLOTS * tok, qrows), bf),
             pltpu.VMEM((SLOTS, 4, tok, dim), f32),
             pltpu.VMEM((SLOTS - 1, 4, tok, dim), bf),
             pltpu.VMEM((SLOTS - 1, 4, tok, dim), bf),
             pltpu.VMEM((GROUPS, qrows, dim), f32),
-            pltpu.VMEM((tok * GROUPS, dim), bf),
-            pltpu.VMEM((tok * GROUPS, dim), bf),
-            pltpu.VMEM((tok, heads, dim), bf),
             pltpu.SemaphoreType.DMA((4,)),
-            pltpu.SemaphoreType.DMA((3,)),
             pltpu.SemaphoreType.DMA((SLOTS - 1, 4)),
             pltpu.SemaphoreType.DMA((SLOTS - 1, 4)),
             pltpu.SemaphoreType.DMA((SLOTS - 1, 4)),
             pltpu.SemaphoreType.DMA((SLOTS - 1, 4)),
         ],
         compiler_params=pltpu.CompilerParams(
-            collective_id=0, has_side_effects=True, vmem_limit_bytes=67_043_328
+            collective_id=0, has_side_effects=True, vmem_limit_bytes=63_000_000
         ),
     )(
         queries,
@@ -353,6 +334,14 @@
         grad_out,
         doc_lengths,
     )
+    dq, dk, dv = pl.pallas_call(
+        writer,
+        out_shape=tuple(jax.ShapeDtypeStruct(shape, bf) for shape in shapes),
+        in_specs=[anywhere] * 3,
+        out_specs=(anywhere,) * 3,
+        scratch_shapes=[pltpu.SemaphoreType.DMA((3,))],
+        compiler_params=pltpu.CompilerParams(vmem_limit_bytes=1_000_000),
+    )(*[pltpu.with_memory_space_constraint(part, pltpu.VMEM) for part in parts])
     return dq, dk.reshape(tok, GROUPS, dim), dv.reshape(tok, GROUPS, dim)
 
 

time: 55.9 us -> 49.5 us (0.89)
  local copies, waits for them, and re-layouts: 3.75 us -> 0 us
  Pallas kernels: 51.3 us -> 48.6 us
    unnamed x7 -> x0, local copies, waits for them, and re-layouts: 3.75 us -> none
    pallas_call x1, Pallas kernels: 51.3 us -> 47.6 us  [local(): pl.pallas_call(functools.partial(kernel, tok, nctx, doc_lengths.shape[0])...]
    pallas_call x0 -> x1, Pallas kernels: none -> 0.96 us  [local(): pl.pallas_call(writer, out_shape=tuple((jax.ShapeDtypeStruct(shape, bf) f...]
where the time goes in v2:
time: 49.5 us; the launch traced here: 49.4 us
  Pallas kernels  48.6 us (98%)
  between operations  0.8 us (2%)
    pallas_call x1, Pallas kernels, local(): pl.pallas_call(functools.partial(kernel, tok, nctx, doc_lengths.shape[0])...  47.6 us

profile of v2, /device:TPU:24, one launch (start us, length us, event | category | flops | bytes accessed | tf_op | source)
XLA Modules:
  0.0 49.4 jit_solution(8404779535779148292)
XLA Ops:
  0.6 47.6 %shard_map.76 = (bf16[192,16,128]{2,1,0:T(8,128)(2,1)S(1)}, bf16[384,128]{1,0:T(8,128)(2,1)S(1)}, bf16[384,128]{1,0:T(8,128)(2,1)S(1)}) custom-call(bf16[192,16,128]{2,1,0:T(8,128)(2,1)} %q_hbm.1, bf16[384,128]{1,0:T(8,128)(2,1)} %bitcast.4, bf16[384,128]{1,0:T(8,128)(2,1)} %bitcast.5, bf16[192,16,128]{2,1,0:T(8,128)(2,1)} %do_hbm.1, s32[64]{0:T(128)} %len_ref.1), custom_call_target="tpu_custom_call" | custom-call | tf_op jit(solution)/shard_map/pallas_call | solution.py:293
  48.3 1.0 %shard_map.77 = (bf16[192,16,128]{2,1,0:T(8,128)(2,1)}, bf16[384,128]{1,0:T(8,128)(2,1)}, bf16[384,128]{1,0:T(8,128)(2,1)}) custom-call(bf16[192,16,128]{2,1,0:T(8,128)(2,1)S(1)} %get-tuple-element.9.a, bf16[384,128]{1,0:T(8,128)(2,1)S(1)} %get-tuple-element.10.b, bf16[384,128]{1,0:T(8,128)(2,1)S(1)} %get-tuple-element.11.c), custom_call_target="tpu_custom_call" | custom-call | tf_op jit(solution)/shard_map/pallas_call | solution.py:337

commit v3 on v2

--- a/solution.py
+++ b/solution.py
@@ -9,6 +9,7 @@
 
 RING = 4
 SLOTS = 8
+RELAY = 8
 FAN = 8
 DIM = 128
 QTILE = 256
@@ -19,13 +20,13 @@
 
 KINDS = ("A", "P", "F", "S", "B", "R", "Q", "O")
 ORDER = (
-    0, 1, 2, 3, 100, 201, 40, 200, 41, 10, 240, 11, 42, 210, 30, 31, 12, 230,
-    43, 50, 32, 241, 51, 250, 70, 33, 231, 13, 71, 211, 21, 20, 220, 60, 52, 270,
-    61, 260, 300, 72, 460, 561, 450, 73, 420, 520, 470, 53, 560, 271, 22, 430, 521, 571,
-    62, 251, 63, 550, 261, 570, 23, 221, 301, 461, 563, 562, 551, 421, 523, 522, 401, 440,
-    471, 573, 531, 451, 553, 410, 511, 572, 431, 552, 530, 441, 411, 510, 400, 630, 533, 541,
-    540, 640, 601, 600, 513, 532, 621, 543, 512, 611, 542, 650, 500, 610, 641, 631, 651, 620,
-    700, 501, 503, 502,
+    0, 1, 2, 3, 100, 201, 200, 40, 41, 240, 42, 11, 43, 10, 241, 31, 30, 12,
+    80, 210, 82, 32, 13, 211, 33, 50, 231, 51, 230, 71, 70, 270, 250, 52, 20, 72,
+    53, 251, 21, 220, 73, 271, 61, 60, 260, 22, 300, 460, 561, 420, 62, 521, 470, 560,
+    63, 520, 23, 261, 221, 301, 421, 523, 461, 562, 571, 450, 551, 522, 563, 451, 471, 550,
+    570, 440, 411, 553, 572, 400, 552, 430, 573, 531, 410, 600, 511, 530, 580, 510, 431, 620,
+    532, 582, 512, 630, 533, 541, 513, 540, 441, 401, 542, 640, 631, 543, 501, 601, 610, 650,
+    621, 641, 500, 651, 502, 611, 700, 503,
 )
 
 
@@ -66,20 +67,25 @@
             kv[g, which, 0:tok] = wide[which, pl.ds(g, tok, stride=GROUPS), :].astype(jnp.bfloat16)
     pl.semaphore_wait(barrier, 4)
 
-    fetch = {
+    common = {
         1: (up, jnp.where(y < RING - 1, 0, 4)),
         2: (up, jnp.where(y < RING - 1, 1, 5)),
         3: (down, jnp.where(y > 0, 4, 0)),
         4: (ahead, 0),
-        5: (ahead, 1),
         6: (down, jnp.where(y > 0, 7, 3)),
-        7: (ahead, 3),
     }
-    parent = {1: down, 2: down, 3: up, 4: behind, 5: behind, 6: up, 7: behind}
+    key_tree = {
+        5: (up, jnp.where(y < RING - 1, 4, RELAY)),
+        7: (down, jnp.where(y > 0, RELAY, 4)),
+        RELAY: (ahead, 4),
+    }
+    fetch = (common | key_tree, common | {5: (ahead, 1), 7: (ahead, 3)})
+    upper = {1: down, 2: down, 3: up, 4: behind, 6: up}
+    parent = (upper | {5: down, 7: up, RELAY: behind}, upper | {5: behind, 7: behind})
 
     def fetch_copy(slot, c):
-        target, source = fetch[slot]
         g, which = c // 2, c % 2
+        target, source = fetch[which][slot]
         rows = pl.ds(pl.multiple_of(source * tok, 16), tok)
         return pltpu.make_async_remote_copy(
             src_ref=kv.at[g, which, rows],
@@ -96,7 +102,7 @@
             dst_ref=rbuf.at[slot - 1, c],
             send_sem=rs_sem.at[slot - 1, c],
             recv_sem=rr_sem.at[slot - 1, c],
-            device_id={"ctx": parent[slot]},
+            device_id={"ctx": parent[c % 2][slot]},
             device_id_type=pl.DeviceIdType.MESH,
         )
 
@@ -109,21 +115,44 @@
             def _():
                 fetch_copy(slot, c).start()
 
-    forwards = {
-        0: ((4, None), (1, y < RING - 1), (3, y == 0)),
-        1: ((5, None), (2, y < RING - 1)),
-        4: ((1, y == RING - 1), (3, y > 0)),
-        3: ((7, None), (6, y == 0)),
-        5: ((2, y == RING - 1),),
-        7: ((6, y > 0),),
-        2: (),
-        6: (),
-    }
+    first = ((4, None), (1, y < RING - 1), (3, y == 0))
+    forwards = (
+        {
+            0: first,
+            1: ((2, y < RING - 1),),
+            4: (
+                (RELAY, y > 0), (1, y == RING - 1), (3, y > 0),
+                (5, y < RING - 1), (7, y == 0),
+            ),
+            3: ((6, y == 0),),
+            5: ((2, y == RING - 1),),
+            7: ((6, y > 0),),
+            RELAY: ((5, y == RING - 1), (7, y > 0)),
+            2: (),
+            6: (),
+        },
+        {
+            0: first,
+            1: ((5, None), (2, y < RING - 1)),
+            4: ((1, y == RING - 1), (3, y > 0)),
+            3: ((7, None), (6, y == 0)),
+            5: ((2, y == RING - 1),),
+            7: ((6, y > 0),),
+            2: (),
+            6: (),
+        },
+    )
 
     def arrive(slot, c):
-        if slot > 0:
+        if slot == RELAY:
+
+            @pl.when(y > 0)
+            def _():
+                fetch_copy(slot, c).wait_recv()
+
+        elif slot > 0:
             fetch_copy(slot, c).wait_recv()
-        for onward, condition in forwards[slot]:
+        for onward, condition in forwards[c % 2][slot]:
             start_if(condition, onward, c)
 
     step = QTILE // FAN
@@ -215,34 +244,34 @@
             grad[slot, 2 * g] = key_sum
             grad[slot, 2 * g + 1] = value_sum
 
-    takes = {
-        7: ((6, y > 0),),
-        5: ((2, y == RING - 1),),
-        3: ((7, None), (6, y == 0)),
-        1: ((5, None), (2, y < RING - 1)),
-        4: ((1, y == RING - 1), (3, y > 0)),
-        0: ((4, None), (1, y < RING - 1), (3, y == 0)),
-    }
-
     def take(slot, given, c):
         return_copy(given, c).wait_recv()
         grad[slot, c] = grad[slot, c] + rbuf[given - 1, c].astype(jnp.float32)
 
     def give_back(slot, c):
-        for given, condition in takes.get(slot, ()):
+        taken = forwards[c % 2][slot]
+        if slot == RELAY:
+            grad[slot, c] = jnp.zeros((tok, DIM), jnp.float32)
+        for given, condition in taken:
             if condition is None:
                 take(slot, given, c)
             else:
                 pl.when(condition)(functools.partial(take, slot, given, c))
-        if slot in takes and slot > 0:
+        if taken and slot > 0:
             sbuf[slot - 1, c] = grad[slot, c].astype(jnp.bfloat16)
-        if slot > 0:
+        if slot == RELAY:
+
+            @pl.when(y > 0)
+            def _():
+                return_copy(slot, c).start()
+
+        elif slot > 0:
             return_copy(slot, c).start()
 
     def query_grads(n, g):
         at = slice(n * QTILE, (n + 1) * QTILE)
         part = lax.dot_general(
-            dscore[g, :, at], kv[g, 0], (((0,), (0,)), ((), ())),
+            dscore[g, :, at], kv[g, 0, 0 : SLOTS * tok], (((0,), (0,)), ((), ())),
             preferred_element_type=jnp.float32,
         )
         dqf[g, at, :] = part * scale
@@ -273,6 +302,12 @@
         for c in range(4):
             fetch_copy(slot, c).wait_send()
             return_copy(slot, c).wait_send()
+
+    @pl.when(y > 0)
+    def _():
+        for c in (0, 2):
+            fetch_copy(RELAY, c).wait_send()
+            return_copy(RELAY, c).wait_send()
 
 
 def writer(a, b, c, out_a, out_b, out_c, sem):
@@ -301,7 +336,7 @@
             pltpu.VMEM((tok * GROUPS, dim), bf),
             pltpu.VMEM((tok * GROUPS, dim), bf),
             pltpu.VMEM((2, tok * GROUPS, dim), f32),
-            pltpu.VMEM((GROUPS, 2, SLOTS * tok, dim), bf),
+            pltpu.VMEM((GROUPS, 2, (SLOTS + 1) * tok, dim), bf),
             pltpu.VMEM((GROUPS, qrows, dim), bf),
             pltpu.VMEM((GROUPS, dim, qrows), bf),
             pltpu.VMEM((GROUPS, qrows, dim), bf),
@@ -314,18 +349,18 @@
             pltpu.VMEM((GROUPS, SLOTS * tok, qrows), f32),
             pltpu.VMEM((GROUPS, SLOTS * tok, qrows), f32),
             pltpu.VMEM((GROUPS, SLOTS * tok, qrows), bf),
-            pltpu.VMEM((SLOTS, 4, tok, dim), f32),
-            pltpu.VMEM((SLOTS - 1, 4, tok, dim), bf),
-            pltpu.VMEM((SLOTS - 1, 4, tok, dim), bf),
+            pltpu.VMEM((SLOTS + 1, 4, tok, dim), f32),
+            pltpu.VMEM((SLOTS, 4, tok, dim), bf),
+            pltpu.VMEM((SLOTS, 4, tok, dim), bf),
             pltpu.VMEM((GROUPS, qrows, dim), f32),
             pltpu.SemaphoreType.DMA((4,)),
-            pltpu.SemaphoreType.DMA((SLOTS - 1, 4)),
-            pltpu.SemaphoreType.DMA((SLOTS - 1, 4)),
-            pltpu.SemaphoreType.DMA((SLOTS - 1, 4)),
-            pltpu.SemaphoreType.DMA((SLOTS - 1, 4)),
+            pltpu.SemaphoreType.DMA((SLOTS, 4)),
+            pltpu.SemaphoreType.DMA((SLOTS, 4)),
+            pltpu.SemaphoreType.DMA((SLOTS, 4)),
+            pltpu.SemaphoreType.DMA((SLOTS, 4)),
         ],
         compiler_params=pltpu.CompilerParams(
-            collective_id=0, has_side_effects=True, vmem_limit_bytes=63_000_000
+            collective_id=0, has_side_effects=True, vmem_limit_bytes=64_500_000
         ),
     )(
         queries,

time: 49.5 us -> 46.8 us (0.945)
  Pallas kernels: 48.6 us -> 45.9 us
    pallas_call x1, Pallas kernels: 47.6 us -> 44.9 us  [local(): pl.pallas_call(functools.partial(kernel, tok, nctx, doc_lengths.shape[0])...]
where the time goes in v3:
time: 46.8 us; the launch traced here: 46.7 us
  Pallas kernels  45.9 us (98%)
  between operations  0.8 us (2%)
    pallas_call x1, Pallas kernels, local(): pl.pallas_call(functools.partial(kernel, tok, nctx, doc_lengths.shape[0])...  44.9 us
    pallas_call x1, Pallas kernels, local(): pl.pallas_call(writer, out_shape=tuple((jax.ShapeDtypeStruct(shape, bf) f...  0.96 us

profile of v3, /device:TPU:24, one launch (start us, length us, event | category | flops | bytes accessed | tf_op | source)
XLA Modules:
  0.0 46.7 jit_solution(17334558634028659807)
XLA Ops:
  0.6 44.9 %shard_map.76 = (bf16[192,16,128]{2,1,0:T(8,128)(2,1)S(1)}, bf16[384,128]{1,0:T(8,128)(2,1)S(1)}, bf16[384,128]{1,0:T(8,128)(2,1)S(1)}) custom-call(bf16[192,16,128]{2,1,0:T(8,128)(2,1)} %q_hbm.1, bf16[384,128]{1,0:T(8,128)(2,1)} %bitcast.4, bf16[384,128]{1,0:T(8,128)(2,1)} %bitcast.5, bf16[192,16,128]{2,1,0:T(8,128)(2,1)} %do_hbm.1, s32[64]{0:T(128)} %len_ref.1), custom_call_target="tpu_custom_call" | custom-call | tf_op jit(solution)/shard_map/pallas_call | solution.py:328
  45.5 1.0 %shard_map.77 = (bf16[192,16,128]{2,1,0:T(8,128)(2,1)}, bf16[384,128]{1,0:T(8,128)(2,1)}, bf16[384,128]{1,0:T(8,128)(2,1)}) custom-call(bf16[192,16,128]{2,1,0:T(8,128)(2,1)S(1)} %get-tuple-element.9.a, bf16[384,128]{1,0:T(8,128)(2,1)S(1)} %get-tuple-element.10.b, bf16[384,128]{1,0:T(8,128)(2,1)S(1)} %get-tuple-element.11.c), custom_call_target="tpu_custom_call" | custom-call | tf_op jit(solution)/shard_map/pallas_call | solution.py:372

commit v4 on v3

--- a/solution.py
+++ b/solution.py
@@ -187,14 +187,19 @@
     last = {0: None, 1: None}
 
     def first_pass(slot, g):
-        rows = slice(slot * tok, (slot + 1) * tok)
-        keys, values = kv[g, 0, rows], kv[g, 1, rows]
         before = last[g]
-        key_pos = (me - slot) * tok + lax.broadcasted_iota(jnp.int32, (tok, QTILE), 0)
         for n in range(tiles):
             at = slice(n * QTILE, (n + 1) * QTILE)
-            scores = jnp.dot(keys, qcol[g, :, at], preferred_element_type=jnp.float32)
-            grads = jnp.dot(values, ocol[g, :, at], preferred_element_type=jnp.float32)
+            low, high = 0, tok
+            if slot == 0:
+                high = (n + 1) * step
+            elif slot == SLOTS - 1:
+                low = n * step
+            rows = slice(slot * tok + low, slot * tok + high)
+            scores = jnp.dot(kv[g, 0, rows], qcol[g, :, at], preferred_element_type=jnp.float32)
+            grads = jnp.dot(kv[g, 1, rows], ocol[g, :, at], preferred_element_type=jnp.float32)
+            key_pos = lax.broadcasted_iota(jnp.int32, (high - low, QTILE), 0)
+            key_pos = key_pos + ((me - slot) * tok + low)
             live = key_pos >= start_ref[:, at]
             if slot == 0:
                 live = live & (key_pos <= pos_ref[:, at])
@@ -215,6 +220,11 @@
             dst_[g : g + 1, at] = dots
             prob[g, rows, at] = probs
             gprob[g, rows, at] = grads
+            for start, stop in ((0, low), (high, tok)):
+                if stop > start:
+                    rest = slice(slot * tok + start, slot * tok + stop)
+                    prob[g, rest, at] = jnp.zeros((stop - start, QTILE), jnp.float32)
+                    gprob[g, rest, at] = jnp.zeros((stop - start, QTILE), jnp.float32)
         last[g] = slot
 
     def statistics(g):

time: 46.8 us -> 46.5 us (level)
  Pallas kernels: 45.9 us -> 45.4 us
where the time goes in v4:
time: 46.5 us; the launch traced here: 46.2 us
  Pallas kernels  45.4 us (98%)
  between operations  0.8 us (2%)
    pallas_call x1, Pallas kernels, local(): pl.pallas_call(functools.partial(kernel, tok, nctx, doc_lengths.shape[0])...  44.5 us
    pallas_call x1, Pallas kernels, local(): pl.pallas_call(writer, out_shape=tuple((jax.ShapeDtypeStruct(shape, bf) f...  0.96 us

profile of v4, /device:TPU:24, one launch (start us, length us, event | category | flops | bytes accessed | tf_op | source)
XLA Modules:
  0.0 46.2 jit_solution(9485808628898318515)
XLA Ops:
  0.6 44.5 %shard_map.76 = (bf16[192,16,128]{2,1,0:T(8,128)(2,1)S(1)}, bf16[384,128]{1,0:T(8,128)(2,1)S(1)}, bf16[384,128]{1,0:T(8,128)(2,1)S(1)}) custom-call(bf16[192,16,128]{2,1,0:T(8,128)(2,1)} %q_hbm.1, bf16[384,128]{1,0:T(8,128)(2,1)} %bitcast.4, bf16[384,128]{1,0:T(8,128)(2,1)} %bitcast.5, bf16[192,16,128]{2,1,0:T(8,128)(2,1)} %do_hbm.1, s32[64]{0:T(128)} %len_ref.1), custom_call_target="tpu_custom_call" | custom-call | tf_op jit(solution)/shard_map/pallas_call | solution.py:338
  45.1 1.0 %shard_map.77 = (bf16[192,16,128]{2,1,0:T(8,128)(2,1)}, bf16[384,128]{1,0:T(8,128)(2,1)}, bf16[384,128]{1,0:T(8,128)(2,1)}) custom-call(bf16[192,16,128]{2,1,0:T(8,128)(2,1)S(1)} %get-tuple-element.9.a, bf16[384,128]{1,0:T(8,128)(2,1)S(1)} %get-tuple-element.10.b, bf16[384,128]{1,0:T(8,128)(2,1)S(1)} %get-tuple-element.11.c), custom_call_target="tpu_custom_call" | custom-call | tf_op jit(solution)/shard_map/pallas_call | solution.py:382
